TPU v7x, 32 devices: a whole 2x2x4 slice. The times are simulated.
32 devices in a mesh: shift: 16 (over z, x, core), row: 2 (over y).
Axes of the slice: x: 2, y: 2, z: 4, core: 2. Of those that a mesh axis runs over, the one named last changes fastest.
Arguments:
- solutions: bfloat16 [32, 2, 2048, 128], P('shift', None, 'row'), may hold values from -96 to 96
Outputs:
- moments: bfloat16 [2, 8, 2048, 128], P(None, None, ('row', 'shift'))
- gram_real: float32 [1024, 1024], replicated
- gram_imag: float32 [1024, 1024], replicated
All inputs are finite; a program needn't handle non-finite values.
Results may differ from a plain program's by a relative error of at most 0.0061.
Values may be sent and summed in bfloat16 or wider, within the bound.
A program may use at most 64 MiB of HBM per device.

v0:
```python
import math
import jax
import jax.numpy as jnp
from jax import lax
from jax.sharding import PartitionSpec as P

PANELS = 8


def coefficient_block(first_shift, shift_count, all_shifts, panels):
    indices = (first_shift + jnp.arange(shift_count, dtype=jnp.int32)).astype(jnp.float32)
    orders = jnp.arange(1, panels + 1, dtype=jnp.int32).astype(jnp.float32)
    angles = orders[:, None] * (2.0 * math.pi * (indices + 0.5) / all_shifts)[None, :]
    cos_part = jnp.cos(angles) / all_shifts
    sin_part = jnp.sin(angles) / all_shifts
    real_row = jnp.stack([cos_part, -sin_part], axis=-1)
    imag_row = jnp.stack([sin_part, cos_part], axis=-1)
    return (
        jnp.stack([real_row, imag_row], axis=0)
        .reshape(2 * panels, 2 * shift_count)
        .astype(jnp.bfloat16)
    )


def weigh(block_data, first_shift, all_shifts):
    shift_count = block_data.shape[0]
    weights = coefficient_block(first_shift, shift_count, all_shifts, PANELS)
    flat = block_data.reshape(2 * shift_count, -1)
    product = jnp.dot(weights, flat, preferred_element_type=jnp.float32)
    return product.reshape(2, PANELS, block_data.shape[2], block_data.shape[3])


def pair_product(left, right):
    width = left.shape[0] * left.shape[2]
    return jnp.einsum("krl,qrm->klqm", left, right, preferred_element_type=jnp.float32).reshape(
        width, width
    )


def gram_terms(moment_block):
    real_part = moment_block[0]
    imag_part = moment_block[1]
    gram_real = pair_product(real_part, real_part) + pair_product(imag_part, imag_part)
    gram_imag = pair_product(real_part, imag_part) - pair_product(imag_part, real_part)
    return (gram_real, gram_imag)


def local(solutions):
    shift_count = solutions.shape[0]
    all_shifts = shift_count * lax.axis_size("shift")
    moment_sum = weigh(
        lax.all_to_all(solutions, "shift", split_axis=2, concat_axis=0, tiled=True), 0, all_shifts
    )
    moments = moment_sum.astype(jnp.bfloat16)
    row_count = moments.shape[2] * lax.axis_size("shift") * lax.axis_size("row")
    shard_real, shard_imag = gram_terms(moments)
    gram_real, gram_imag = lax.psum((shard_real, shard_imag), ("shift", "row"))
    factor = 1.0 / math.sqrt(row_count)
    return (moments, gram_real * factor, gram_imag * factor)


def solution(mesh):
    placed = (P("shift", None, "row", None),)
    return jax.shard_map(
        local,
        mesh=mesh,
        in_specs=placed,
        out_specs=(P(None, None, ("row", "shift"), None), P(), P()),
        check_vma=False,
    )
```

profile of v0, /device:TPU:0, one launch (start us, length us, event | category | flops | bytes accessed | tf_op | source)
XLA Modules:
  0.0 245.7 jit_solution(16448146008260359767)
XLA Ops:
  7.2 3.3 %copy.14 = bf16[2,2,1024,128]{3,1,0,2:T(2,128)(2,1)} copy(bf16[2,2,1024,128]{3,2,1,0:T(8,128)(2,1)} %param.1) | data formatting | bytes 2097152 | tf_op args[0]
  10.4 7.4 %all-to-all-start = ((bf16[2,2,1024,128]{3,1,0,2:T(2,128)(2,1)}), bf16[2,2,1024,128]{3,1,0,2:T(2,128)(2,1)S(1)}, u32[]{:S(2)}, u32[]{:S(2)}) async-start(bf16[2,2,1024,128]{3,1,0,2:T(2,128)(2,1)} %copy.14), calls=%async_computation | async-start | bytes 2097152 | tf_op jit(solution)/shard_map/all_to_all | solution.py:52
  17.8 0.0 all-reduce.3.cloned.1.call-start
  17.9 0.1 fusion.20
  18.0 0.1 copy.10
  18.1 0.1 copy.12
  18.2 0.1 copy.11
  18.3 0.1 copy.13
  18.4 22.3 %all-to-all-done = bf16[2,2,1024,128]{3,1,0,2:T(2,128)(2,1)S(1)} async-done(((bf16[2,2,1024,128]{3,1,0,2:T(2,128)(2,1)}), bf16[2,2,1024,128]{3,1,0,2:T(2,128)(2,1)S(1)}, u32[]{:S(2)}, u32[]{:S(2)}) %all-to-all-start) | async-done | bytes 1048608 | tf_op jit(solution)/shard_map/all_to_all | solution.py:52
  40.7 0.3 copy.15
  41.0 0.7 convolution_convert_fusion
  41.7 0.7 fusion.7
  42.4 0.7 fusion.2
  43.2 2.8 %convolution_subtract_fusion = f32[1024,1024]{1,0:T(8,128)} fusion(f32[1024,1024]{1,0:T(8,128)S(1)} %fusion.2, bf16[8,8,8,128]{3,2,1,0:T(8,128)(2,1)S(1)} %bitcast.54, bf16[8,8,8,128]{3,2,1,0:T(8,128)(2,1)S(1)} %bitcast.58), kind=kOutput, calls=%fused_computation | convolution fusion | flops 135266304 | bytes 8650752 | tf_op jit(solution)/shard_map/krl,qrm->klqm/dot_general | solution.py:35
  45.9 2.7 %convolution_add_fusion = f32[1024,1024]{1,0:T(8,128)} fusion(f32[1024,1024]{1,0:T(8,128)S(1)} %fusion.7, bf16[8,8,8,128]{3,2,1,0:T(8,128)(2,1)S(1)} %bitcast.55), kind=kOutput, calls=%fused_computation.1 | convolution fusion | flops 135266304 | bytes 8519680 | tf_op jit(solution)/shard_map/krl,qrm->klqm/dot_general | solution.py:35
  48.6 0.0 all-reduce.3.cloned.1.call-update
  48.7 0.8 copy.17
  49.4 180.6 %all-reduce.3.cloned.1.call-done = (f32[1024,1024]{1,0:T(8,128)}, f32[1024,1024]{1,0:T(8,128)}) async-done(((f32[1024,1024]{1,0:T(8,128)}, f32[1024,1024]{1,0:T(8,128)}), (f32[1024,1024]{1,0:T(8,128)}, f32[1024,1024]{1,0:T(8,128)})) %all-reduce.3.cloned.1.call-update) | async-done | bytes 8388624 | tf_op jit(solution)/shard_map/psum | solution.py:57
  230.0 8.9 %broadcast_multiply_fusion = (f32[1024,1024]{1,0:T(8,128)}, f32[1024,1024]{1,0:T(8,128)}) fusion(f32[1024,1024]{1,0:T(8,128)} %get-tuple-element.13, f32[1024,1024]{1,0:T(8,128)} %get-tuple-element.12), kind=kLoop, calls=%fused_computation.2 | loop fusion | flops 2097152 | bytes 16777216 | tf_op jit(solution)/shard_map/mul | solution.py:59
  (4 shorter events, 0.0 us)
Async XLA Ops:
  10.4 30.3 %all-to-all-start = ((bf16[2,2,1024,128]{3,1,0,2:T(2,128)(2,1)}), bf16[2,2,1024,128]{3,1,0,2:T(2,128)(2,1)S(1)}, u32[]{:S(2)}, u32[]{:S(2)}) async-start(bf16[2,2,1024,128]{3,1,0,2:T(2,128)(2,1)} %copy.14), calls=%async_computation | async-start | bytes 2097152 | tf_op jit(solution)/shard_map/all_to_all | solution.py:52
  17.8 212.2 %all-reduce.3.cloned.1.call-start = ((), (), s32[]{:S(2)}) async-start(), calls=%async_computation.1 | async-start | bytes 16777216 | tf_op jit(solution)/shard_map/psum | solution.py:57
Sparse Core Ops, SparseCore 0:
  48.8 181.2 all-reduce.2
where the time goes:
time: 246 us
  waiting for transfers between devices  203 us (83%)
  between operations  14.1 us (6%)
  other arithmetic  8.99 us (4%)
  matrix products  7.62 us (3%)
  starting transfers between devices  7.43 us (3%)
  local copies, waits for them, and re-layouts  4.65 us (2%)
    psum x1, waiting for transfers between devices, local(): gram_real, gram_imag = lax.psum((shard_real, shard_imag), ('shift', 'row'))  181 us
    all_to_all x1, waiting for transfers between devices, local(): lax.all_to_all(solutions, 'shift', split_axis=2, concat_axis=0, tiled=True)  22.3 us
    mul x1, other arithmetic, local(): return (moments, gram_real * factor, gram_imag * factor)  8.85 us
    all_to_all x1, starting transfers between devices, local(): lax.all_to_all(solutions, 'shift', split_axis=2, concat_axis=0, tiled=True)  7.39 us
    dot_general x4, matrix products, pair_product(): jnp.einsum('krl,qrm->klqm', left, right, preferred_element_type=jnp.float32)  6.95 us
  transfers between devices with their start and end apart: 2, of which 2 were waited for; matrix products, arithmetic and copies ran while one was open for 0% of the time, Pallas kernels for 0%

commit v1 on v0

--- a/solution.py
+++ b/solution.py
@@ -48,9 +48,13 @@
 def local(solutions):
     shift_count = solutions.shape[0]
     all_shifts = shift_count * lax.axis_size("shift")
-    moment_sum = weigh(
-        lax.all_to_all(solutions, "shift", split_axis=2, concat_axis=0, tiled=True), 0, all_shifts
+    supply_ways_over_axis = lambda group_axis, incoming_x: jnp.concatenate(
+        lax.all_to_all(
+            jnp.stack(jnp.split(incoming_x, lax.axis_size(group_axis), axis=2)), group_axis, 0, 0
+        ),
+        axis=0,
     )
+    moment_sum = weigh(supply_ways_over_axis("shift", solutions), 0, all_shifts)
     moments = moment_sum.astype(jnp.bfloat16)
     row_count = moments.shape[2] * lax.axis_size("shift") * lax.axis_size("row")
     shard_real, shard_imag = gram_terms(moments)

time: 246 us -> 267 us (1.085)
  local copies, waits for them, and re-layouts: 4.65 us -> 24.7 us
    unnamed x2 -> x16, local copies, waits for them, and re-layouts: 4.03 us -> 22.9 us
where the time goes in v1:
time: 267 us; the launch traced here: 266 us
  waiting for transfers between devices  203 us (76%)
  local copies, waits for them, and re-layouts  24.7 us (9%)
  between operations  14.1 us (5%)
  other arithmetic  8.99 us (3%)
  matrix products  7.61 us (3%)
  starting transfers between devices  7.43 us (3%)
    psum x1, waiting for transfers between devices, local(): gram_real, gram_imag = lax.psum((shard_real, shard_imag), ('shift', 'row'))  181 us
    unnamed x16, local copies, waits for them, and re-layouts  22.9 us
    all_to_all x1, waiting for transfers between devices, local(): lax.all_to_all(jnp.stack(jnp.split(incoming_x, lax.axis_size(group_axis),...  22.3 us
    mul x1, other arithmetic, local(): return (moments, gram_real * factor, gram_imag * factor)  8.85 us
    all_to_all x1, starting transfers between devices, local(): lax.all_to_all(jnp.stack(jnp.split(incoming_x, lax.axis_size(group_axis),...  7.39 us
    dot_general x4, matrix products, pair_product(): jnp.einsum('krl,qrm->klqm', left, right, preferred_element_type=jnp.float32)  6.95 us
  transfers between devices with their start and end apart: 2, of which 2 were waited for; matrix products, arithmetic and copies ran while one was open for 0% of the time, Pallas kernels for 0%

profile of v1, /device:TPU:0, one launch (start us, length us, event | category | flops | bytes accessed | tf_op | source)
XLA Modules:
  0.0 265.8 jit_solution(7049309099060135210)
XLA Ops:
  7.2 1.5 bitcast_dynamic-update-slice_fusion.15
  8.6 1.5 bitcast_dynamic-update-slice_fusion.14
  10.1 1.5 bitcast_dynamic-update-slice_fusion.13
  11.6 1.5 bitcast_dynamic-update-slice_fusion.12
  13.1 1.5 bitcast_dynamic-update-slice_fusion.11
  14.5 1.5 bitcast_dynamic-update-slice_fusion.10
  16.0 1.5 bitcast_dynamic-update-slice_fusion.9
  17.5 1.5 bitcast_dynamic-update-slice_fusion.8
  19.0 1.5 bitcast_dynamic-update-slice_fusion.7
  20.4 1.5 bitcast_dynamic-update-slice_fusion.6
  21.9 1.5 bitcast_dynamic-update-slice_fusion.5
  23.4 1.5 bitcast_dynamic-update-slice_fusion.4
  24.9 1.5 bitcast_dynamic-update-slice_fusion.3
  26.3 1.5 bitcast_dynamic-update-slice_fusion.2
  27.8 1.5 bitcast_dynamic-update-slice_fusion.1
  29.3 1.5 bitcast_dynamic-update-slice_fusion
  30.7 7.4 %all-to-all-start = ((bf16[16,2,2,64,128]{4,3,2,1,0:T(8,128)(2,1)}), bf16[16,2,2,64,128]{4,3,2,1,0:T(8,128)(2,1)S(1)}, u32[]{:S(2)}, u32[]{:S(2)}) async-start(bf16[16,2,2,64,128]{4,3,2,1,0:T(8,128)(2,1)} %bitcast_dynamic-update-slice_fusion), calls=%async_computation | async-start | bytes 2097152 | tf_op jit(solution)/shard_map/all_to_all | solution.py:52
  38.1 0.0 all-reduce.3.cloned.1.call-start
  38.2 0.1 fusion.20
  38.3 0.1 copy.9
  38.4 0.1 copy.11
  38.5 0.1 copy.10
  38.6 0.1 copy.12
  38.7 22.3 %all-to-all-done = bf16[16,2,2,64,128]{4,3,2,1,0:T(8,128)(2,1)S(1)} async-done(((bf16[16,2,2,64,128]{4,3,2,1,0:T(8,128)(2,1)}), bf16[16,2,2,64,128]{4,3,2,1,0:T(8,128)(2,1)S(1)}, u32[]{:S(2)}, u32[]{:S(2)}) %all-to-all-start) | async-done | bytes 1048608 | tf_op jit(solution)/shard_map/all_to_all | solution.py:52
  61.0 0.7 convolution_convert_fusion
  61.7 0.7 fusion.7
  62.4 0.7 fusion.2
  63.2 2.7 %convolution_subtract_fusion = f32[1024,1024]{1,0:T(8,128)} fusion(f32[1024,1024]{1,0:T(8,128)S(1)} %fusion.2, bf16[8,8,8,128]{3,2,1,0:T(8,128)(2,1)S(1)} %bitcast.83, bf16[8,8,8,128]{3,2,1,0:T(8,128)(2,1)S(1)} %bitcast.87), kind=kOutput, calls=%fused_computation | convolution fusion | flops 135266304 | bytes 8650752 | tf_op jit(solution)/shard_map/krl,qrm->klqm/dot_general | solution.py:35
  65.9 2.7 %convolution_add_fusion = f32[1024,1024]{1,0:T(8,128)} fusion(f32[1024,1024]{1,0:T(8,128)S(1)} %fusion.7, bf16[8,8,8,128]{3,2,1,0:T(8,128)(2,1)S(1)} %bitcast.84), kind=kOutput, calls=%fused_computation.1 | convolution fusion | flops 135266304 | bytes 8519680 | tf_op jit(solution)/shard_map/krl,qrm->klqm/dot_general | solution.py:35
  68.7 0.0 all-reduce.3.cloned.1.call-update
  68.7 0.8 copy.14
  69.5 180.6 %all-reduce.3.cloned.1.call-done = (f32[1024,1024]{1,0:T(8,128)}, f32[1024,1024]{1,0:T(8,128)}) async-done(((f32[1024,1024]{1,0:T(8,128)}, f32[1024,1024]{1,0:T(8,128)}), (f32[1024,1024]{1,0:T(8,128)}, f32[1024,1024]{1,0:T(8,128)})) %all-reduce.3.cloned.1.call-update) | async-done | bytes 8388624 | tf_op jit(solution)/shard_map/psum | solution.py:61
  250.1 8.9 %broadcast_multiply_fusion = (f32[1024,1024]{1,0:T(8,128)}, f32[1024,1024]{1,0:T(8,128)}) fusion(f32[1024,1024]{1,0:T(8,128)} %get-tuple-element.13, f32[1024,1024]{1,0:T(8,128)} %get-tuple-element.12), kind=kLoop, calls=%fused_computation.2 | loop fusion | flops 2097152 | bytes 16777216 | tf_op jit(solution)/shard_map/mul | solution.py:63
  (4 shorter events, 0.0 us)
Async XLA Ops:
  30.7 30.3 %all-to-all-start = ((bf16[16,2,2,64,128]{4,3,2,1,0:T(8,128)(2,1)}), bf16[16,2,2,64,128]{4,3,2,1,0:T(8,128)(2,1)S(1)}, u32[]{:S(2)}, u32[]{:S(2)}) async-start(bf16[16,2,2,64,128]{4,3,2,1,0:T(8,128)(2,1)} %bitcast_dynamic-update-slice_fusion), calls=%async_computation | async-start | bytes 2097152 | tf_op jit(solution)/shard_map/all_to_all | solution.py:52
  38.1 211.9 %all-reduce.3.cloned.1.call-start = ((), (), s32[]{:S(2)}) async-start(), calls=%async_computation.1 | async-start | bytes 16777216 | tf_op jit(solution)/shard_map/psum | solution.py:61
Sparse Core Ops, SparseCore 0:
  68.8 181.2 all-reduce.2

commit v2 on v0

--- a/solution.py
+++ b/solution.py
@@ -5,6 +5,12 @@
 from jax.sharding import PartitionSpec as P
 
 PANELS = 8
+
+
+def clear_edge(payload, link_axis, mesh_dim="shift"):
+    for dev_j in (link_axis, mesh_dim):
+        payload = lax.psum(payload, dev_j)
+    return payload
 
 
 def coefficient_block(first_shift, shift_count, all_shifts, panels):
@@ -54,7 +60,7 @@
     moments = moment_sum.astype(jnp.bfloat16)
     row_count = moments.shape[2] * lax.axis_size("shift") * lax.axis_size("row")
     shard_real, shard_imag = gram_terms(moments)
-    gram_real, gram_imag = lax.psum((shard_real, shard_imag), ("shift", "row"))
+    gram_real, gram_imag = clear_edge((shard_real, shard_imag), "row")
     factor = 1.0 / math.sqrt(row_count)
     return (moments, gram_real * factor, gram_imag * factor)
 

time: 246 us -> 439 us (1.78)
  waiting for transfers between devices: 203 us -> 396 us
    psum x1 -> x2, waiting for transfers between devices: 181 us -> 374 us  [clear_edge(): payload = lax.psum(payload, dev_j)]
  transfers between devices with their start and end apart: 2 -> 3, of which waited for: 2 -> 3; matrix products, arithmetic and copies ran while one was open for 0% -> 0% of each run, Pallas kernels for 0% -> 0%
where the time goes in v2:
time: 439 us
  waiting for transfers between devices  396 us (90%)
  between operations  14.1 us (3%)
  other arithmetic  8.99 us (2%)
  matrix products  7.62 us (2%)
  starting transfers between devices  7.47 us (2%)
  local copies, waits for them, and re-layouts  4.65 us (1%)
    psum x2, waiting for transfers between devices, clear_edge(): payload = lax.psum(payload, dev_j)  374 us
    all_to_all x1, waiting for transfers between devices, local(): lax.all_to_all(solutions, 'shift', split_axis=2, concat_axis=0, tiled=True)  22.3 us
    mul x1, other arithmetic, local(): return (moments, gram_real * factor, gram_imag * factor)  8.85 us
  transfers between devices with their start and end apart: 3, of which 3 were waited for; matrix products, arithmetic and copies ran while one was open for 0% of the time, Pallas kernels for 0%

profile of v2, /device:TPU:0, one launch (start us, length us, event | category | flops | bytes accessed | tf_op | source)
XLA Modules:
  0.0 439.0 jit_solution(12760115862139067368)
XLA Ops:
  7.2 3.3 copy.14
  10.4 7.4 %all-to-all-start = ((bf16[2,2,1024,128]{3,1,0,2:T(2,128)(2,1)}), bf16[2,2,1024,128]{3,1,0,2:T(2,128)(2,1)S(1)}, u32[]{:S(2)}, u32[]{:S(2)}) async-start(bf16[2,2,1024,128]{3,1,0,2:T(2,128)(2,1)} %copy.14), calls=%async_computation | async-start | bytes 2097152 | tf_op jit(solution)/shard_map/all_to_all | solution.py:58
  17.8 0.0 all-reduce.7.cloned.1.call-start
  17.9 0.1 fusion.20
  18.0 0.1 copy.10
  18.1 0.1 copy.12
  18.2 0.1 copy.11
  18.3 0.1 copy.13
  18.4 22.3 %all-to-all-done = bf16[2,2,1024,128]{3,1,0,2:T(2,128)(2,1)S(1)} async-done(((bf16[2,2,1024,128]{3,1,0,2:T(2,128)(2,1)}), bf16[2,2,1024,128]{3,1,0,2:T(2,128)(2,1)S(1)}, u32[]{:S(2)}, u32[]{:S(2)}) %all-to-all-start) | async-done | bytes 1048608 | tf_op jit(solution)/shard_map/all_to_all | solution.py:58
  40.7 0.3 copy.15
  41.0 0.7 convolution_convert_fusion
  41.7 0.7 fusion.7
  42.4 0.7 fusion.2
  43.2 2.8 convolution_subtract_fusion
  45.9 2.7 convolution_add_fusion
  48.6 0.0 all-reduce.7.cloned.1.call-update
  48.7 0.0 all-reduce.5.cloned.1.call-start
  48.7 200.3 %all-reduce.7.cloned.1.call-done = (f32[1024,1024]{1,0:T(8,128)}, f32[1024,1024]{1,0:T(8,128)}) async-done(((f32[1024,1024]{1,0:T(8,128)}, f32[1024,1024]{1,0:T(8,128)}), (f32[1024,1024]{1,0:T(8,128)}, f32[1024,1024]{1,0:T(8,128)})) %all-reduce.7.cloned.1.call-update) | async-done | bytes 8388624 | tf_op jit(solution)/shard_map/psum | solution.py:12
  249.1 0.0 all-reduce.5.cloned.1.call-update
  249.1 0.8 copy.17
  249.8 173.5 %all-reduce.5.cloned.1.call-done = (f32[1024,1024]{1,0:T(8,128)}, f32[1024,1024]{1,0:T(8,128)}) async-done(((f32[1024,1024]{1,0:T(8,128)}, f32[1024,1024]{1,0:T(8,128)}), (f32[1024,1024]{1,0:T(8,128)}, f32[1024,1024]{1,0:T(8,128)})) %all-reduce.5.cloned.1.call-update) | async-done | bytes 8388624 | tf_op jit(solution)/shard_map/psum | solution.py:12
  423.3 8.9 %broadcast_multiply_fusion = (f32[1024,1024]{1,0:T(8,128)}, f32[1024,1024]{1,0:T(8,128)}) fusion(f32[1024,1024]{1,0:T(8,128)} %get-tuple-element.13, f32[1024,1024]{1,0:T(8,128)} %get-tuple-element.12), kind=kLoop, calls=%fused_computation.2 | loop fusion | flops 2097152 | bytes 16777216 | tf_op jit(solution)/shard_map/mul | solution.py:65
  (4 shorter events, 0.0 us)
Async XLA Ops:
  10.4 30.3 %all-to-all-start = ((bf16[2,2,1024,128]{3,1,0,2:T(2,128)(2,1)}), bf16[2,2,1024,128]{3,1,0,2:T(2,128)(2,1)S(1)}, u32[]{:S(2)}, u32[]{:S(2)}) async-start(bf16[2,2,1024,128]{3,1,0,2:T(2,128)(2,1)} %copy.14), calls=%async_computation | async-start | bytes 2097152 | tf_op jit(solution)/shard_map/all_to_all | solution.py:58
  17.8 231.2 %all-reduce.7.cloned.1.call-start = ((), (), s32[]{:S(2)}) async-start(), calls=%async_computation.2 | async-start | bytes 16777216 | tf_op jit(solution)/shard_map/psum | solution.py:12
  48.7 374.6 %all-reduce.5.cloned.1.call-start = ((), (), s32[]{:S(2)}) async-start(), calls=%async_computation.1 | async-start | bytes 16777216 | tf_op jit(solution)/shard_map/psum | solution.py:12
Sparse Core Ops, SparseCore 0:
  48.8 200.2 all-reduce.6
  252.8 170.4 all-reduce.4
